TPU v7x, 32 devices: a whole 2x2x4 slice. The times are simulated.
32 devices in a mesh: width: 8 (over z, core), lat: 4 (over y, x).
Axes of the slice: x: 2, y: 2, z: 4, core: 2. Of those that a mesh axis runs over, the one named last changes fastest.
Arguments:
- residuals: bfloat16 [384, 16384], P(None, 'width'), may hold values from -6 to 6
- encoder: bfloat16 [16384, 4096], P('width', 'lat'), may hold values from -0.046875 to 0.046875
- enc_bias: float32 [4096], P('lat'), may hold values from -3 to 3
- decoder: bfloat16 [4096, 16384], P('lat', 'width'), may hold values from -0.046875 to 0.046875
- dec_bias: float32 [16384], P('width'), may hold values from -3 to 3
Outputs:
- enc_grad: bfloat16 [16384, 4096], P('width', 'lat')
- new_decoder: bfloat16 [4096, 16384], P('lat', 'width')
All inputs are finite; a program needn't handle non-finite values.
Results may differ from a plain program's by a relative error of at most 0.011.
Values may be sent and summed in bfloat16 or wider, within the bound.
A program may use at most 64 MiB of HBM per device.

v0:
```python
import functools

import jax
import jax.numpy as jnp
from jax import lax
from jax.experimental import pallas as pl
from jax.experimental.pallas import tpu as pltpu
from jax.sharding import PartitionSpec as P

EPS = 1e-06
STEP = 0.0003
PENALTY = 0.5
MESH = pl.DeviceIdType.MESH
F32, BF16 = jnp.float32, jnp.bfloat16
NT = (((1,), (1,)), ((), ()))


def step_kernel(
    Z, NL, NK, NN,
    res_h, enc_h, bias, dec_h, dbias,
    nd_o, dp_o, rt_o,
    res_v, enc_v, dec_v, stA, rxA, sA, rA, preS, acts, actsT, rt_v,
    rf, sB, rB, err, dacc, sD, rxD, sS, rD, dp, grad, sacc, stv, rst, ss, rs2, nd_v,
    in_sem, out_sem,
    a1s, a1r, a2s, a2r, a3s, a3r, a4s, a4r,
    bs, br, cs, cr,
    d1s, d1r, d2s, d2r, d3s, d3r, d4s, d4r,
    e1s, e1r, e2s, e2r,
):
    T, DW = res_v.shape
    H = acts.shape[0]
    TH = T // H
    TB, KC = acts.shape[-2:]
    KB = 2 * KC
    TL, NB = err.shape[-2:]
    w = lax.axis_index("width")
    l = lax.axis_index("lat")
    z, c = w // 2, w % 2
    pc = 1 - c
    partner = (z * 2 + pc, l)

    def zdev(o):
        return ((z + o) % Z) * 2 + c, l

    def lat_to(o):
        return ((l // 2 + o // 2) % (NL // 2)) * 2 + (l % 2 + o % 2) % 2

    def lat_from(o):
        return ((l // 2 + NL // 2 - o // 2) % (NL // 2)) * 2 + (l % 2 + o % 2) % 2

    def rc(src, dst, ssem, rsem, dev):
        return pltpu.make_async_remote_copy(
            src_ref=src, dst_ref=dst, send_sem=ssem, recv_sem=rsem,
            device_id=dev, device_id_type=MESH,
        )

    def loop(n, f):
        lax.fori_loop(0, n, lambda i, _: (f(i), 0)[1], 0)

    c_res = pltpu.make_async_copy(res_h, res_v, in_sem.at[0])
    c_res.start()

    def enc_copy(k):
        return pltpu.make_async_copy(
            enc_h.at[:, pl.ds(pl.multiple_of(k * KB, KB), KB)], enc_v.at[k], in_sem.at[1 + k]
        )

    def dec_copy(n):
        return pltpu.make_async_copy(
            dec_h.at[:, pl.ds(pl.multiple_of(n * NB, NB), NB)], dec_v.at[n], in_sem.at[1 + NK + n]
        )

    for k in range(NK):
        enc_copy(k).start()
    for n in range(NN):
        dec_copy(n).start()

    barrier = pltpu.get_barrier_semaphore()
    pl.semaphore_signal(barrier, inc=1, device_id=partner, device_id_type=MESH)
    for o in range(1, Z):
        pl.semaphore_signal(barrier, inc=1, device_id=zdev(o), device_id_type=MESH)
    for o in range(1, NL):
        pl.semaphore_signal(barrier, inc=1, device_id=(w, lat_to(o)), device_id_type=MESH)

    def a1(h, k):
        return rc(stA.at[h, k, pc], rxA.at[h, k], a1s.at[h, k], a1r.at[h, k], partner)

    def a2(h, k, o):
        return rc(
            sA.at[h, k, (z + o) % Z], rA.at[h, k, o], a2s.at[h, k, o], a2r.at[h, k, o], zdev(o)
        )

    def own_z(ref, ssem, rsem):
        def send(h, k, o):
            block = ref.at[h, k, c, z]
            return rc(block, block, ssem.at[h, k, o], rsem.at[h, k, o], zdev(o))

        def arrive(h, k, o):
            block = ref.at[h, k, c, (z + Z - o) % Z]
            return rc(block, block, ssem.at[h, k, o], rsem.at[h, k, o], zdev(o))

        return send, arrive

    def own_core(ref, ssem, rsem):
        def send(h, k):
            block = ref.at[h, k, c]
            return rc(block, block, ssem.at[h, k], rsem.at[h, k], partner)

        def arrive(h, k):
            block = ref.at[h, k, pc]
            return rc(block, block, ssem.at[h, k], rsem.at[h, k], partner)

        return send, arrive

    a3, a3in = own_z(acts, a3s, a3r)
    a4, a4in = own_core(acts, a4s, a4r)
    d3, d3in = own_z(dp, d3s, d3r)
    d4, d4in = own_core(dp, d4s, d4r)

    def combine_a(h, k):
        a1(h, k).wait_recv()
        sA[h, k] = stA[h, k, c] + rxA[h, k]
        for o in range(1, Z):
            a2(h, k, o).start()

    c_res.wait()
    pl.semaphore_wait(barrier, 1 + (Z - 1) + (NL - 1))

    def pre_part(h, k):
        p = jnp.dot(res_v[h * TH:(h + 1) * TH, :], enc_v[k], preferred_element_type=F32)
        for j in range(2):
            stA[h, k, j] = p[:, j * KC:(j + 1) * KC].reshape(Z, TB, KC)
        a1(h, k).start()

    def pre_first(k):
        enc_copy(k).wait()
        pre_part(0, k)

        @pl.when(k > 0)
        def _():
            combine_a(0, k - 1)

    loop(NK, pre_first)
    combine_a(0, NK - 1)
    for h in range(1, H):
        loop(NK, lambda k: pre_part(h, k))

    def fwd_a(h, k):
        for o in range(1, Z):
            a3in(h, k, o).wait_recv()
        a4(h, k).start()

    def act_step(h, k):
        for o in range(1, Z):
            a2(h, k, o).wait_recv()
        pre = sA[h, k, z]
        for o in range(1, Z):
            pre = pre + rA[h, k, o]
        pre = pre + bias[k, c]
        preS[h, k] = pre
        acts[h, k, c, z] = jnp.maximum(pre, 0.0).astype(BF16)
        for o in range(1, Z):
            a3(h, k, o).start()

    loop(NK, lambda k: act_step(0, k))
    loop(NK, lambda k: combine_a(1, k))

    def rt_step(n):
        rt_v[n] = res_v[:, pl.ds(pl.multiple_of(n * NB, NB), NB)].T

    loop(NN, rt_step)
    rt_copy = pltpu.make_async_copy(rt_v, rt_o, out_sem.at[0])
    rt_copy.start()

    def b1(h, n, o):
        to = lat_to(o)
        return rc(sB.at[h, n, to], rB.at[h, n, o], bs.at[h, n, o], br.at[h, n, o], (w, to))

    def c1(h, n, o):
        block = err.at[h, n, l]
        return rc(block, block, cs.at[h, n, o], cr.at[h, n, o], (w, lat_to(o)))

    def c1in(h, n, o):
        block = err.at[h, n, lat_from(o)]
        return rc(block, block, cs.at[h, n, o], cr.at[h, n, o], (w, lat_to(o)))

    def rec_step(h, n):
        a = jnp.concatenate(
            [acts[h, k, j].reshape(TH, KC) for k in range(NK) for j in range(2)], axis=1
        )
        r = jnp.dot(a, dec_v[n], preferred_element_type=F32).reshape(NL, TL, NB)
        rf[h, n] = r
        sB[h, n] = r.astype(BF16)
        for o in range(1, NL):
            b1(h, n, o).start()

    def at_step(h, k):
        a = jnp.concatenate([acts[h, k, j].reshape(TH, KC) for j in range(2)], axis=1)
        actsT[h, k] = a.T

    def err_step(h, n):
        for o in range(1, NL):
            b1(h, n, o).wait_recv()
        r = rf[h, n, l]
        for o in range(1, NL):
            r = r + rB[h, n, o].astype(F32)
        own = res_v[
            pl.ds(pl.multiple_of(h * TH + l * TL, TL), TL),
            pl.ds(pl.multiple_of(n * NB, NB), NB),
        ]
        err[h, n, l] = (r + dbias[n] - own.astype(F32)).astype(BF16)
        for o in range(1, NL):
            c1(h, n, o).start()

    def recon(h):
        loop(NK, lambda k: fwd_a(h, k))
        if h == 0:
            for n in range(NN):
                dec_copy(n).wait()
        loop(NK, lambda k: a4in(h, k).wait_recv())
        loop(NN, lambda n: rec_step(h, n))
        loop(NK, lambda k: at_step(h, k))

    recon(0)

    def zero_step(k):
        for s in range(3):
            sacc[s, k] = jnp.zeros(sacc.shape[2:], F32)

    loop(NK, zero_step)

    def err_act(i):
        err_step(0, i)
        act_step(1, i)

    loop(NK, err_act)
    recon(1)

    def dec_rows(n, k):
        return dec_v[n, pl.ds(pl.multiple_of(k * KB, KB), KB), :]

    def dacts_part(h, n, k):
        d = lax.dot_general(
            err[h, n].reshape(TH, NB), dec_rows(n, k), NT, preferred_element_type=F32
        )
        return [d[:, j * KC:(j + 1) * KC].reshape(Z, TB, KC) for j in range(2)]

    def grad_first(n, k):
        grad[n, k] = jnp.dot(
            actsT[0, k], err[0, n].reshape(TH, NB), preferred_element_type=F32
        )

    def grad_last(n, k):
        g = grad[n, k] + jnp.dot(
            actsT[1, k], err[1, n].reshape(TH, NB), preferred_element_type=F32
        )
        grad[n, k] = g
        wt = dec_rows(n, k).astype(F32)
        for s, prod in enumerate((wt * wt, g * wt, g * g)):
            part = prod[:, 0:128]
            for j in range(1, NB // 128):
                part = part + prod[:, j * 128:(j + 1) * 128]
            sacc[s, k] += part

    def err_wait(h, n):
        for o in range(1, NL):
            c1in(h, n, o).wait_recv()

    def d1(h, k):
        return rc(sD.at[h, k, pc], rxD.at[h, k], d1s.at[h, k], d1r.at[h, k], partner)

    def d2(h, k, o):
        return rc(
            sS.at[h, k, (z + o) % Z], rD.at[h, k, o], d2s.at[h, k, o], d2r.at[h, k, o], zdev(o)
        )

    def combine_d(h, k):
        d1(h, k).wait_recv()
        s = dacc[h, k, c] + rxD[h, k].astype(F32)
        dacc[h, k, c] = s
        sS[h, k] = s.astype(BF16)
        for o in range(1, Z):
            d2(h, k, o).start()

    def dacts_add(h, n, k):
        for j, d in enumerate(dacts_part(h, n, k)):
            if isinstance(n, int) and n == 0:
                dacc[h, k, j] = d
            else:
                dacc[h, k, j] += d

    last = NN - 1

    def d_step(h, k):
        for j, d in enumerate(dacts_part(h, last, k)):
            v = dacc[h, k, j] + d
            dacc[h, k, j] = v
            sD[h, k, j] = v.astype(BF16)
        d1(h, k).start()

        @pl.when(k > 0)
        def _():
            combine_d(h, k - 1)

    def dacts(h, beside):
        def step(n):
            err_wait(h, n)

            def k_step(k):
                dacts_add(h, n, k)
                beside(n, k)

            loop(NK, k_step)

        step(0)
        lax.fori_loop(1, last, lambda n, _: (step(n), 0)[1], 0)
        err_wait(h, last)
        loop(NK, lambda k: d_step(h, k))
        combine_d(h, NK - 1)

    def dp_step(h, k):
        for o in range(1, Z):
            d2(h, k, o).wait_recv()
        v = dacc[h, k, c, z]
        for o in range(1, Z):
            v = v + rD[h, k, o].astype(F32)
        dp[h, k, c, z] = jnp.where(preS[h, k] > 0.0, v + PENALTY, 0.0).astype(BF16)
        for o in range(1, Z):
            d3(h, k, o).start()

    def fwd_d(h, k):
        for o in range(1, Z):
            d3in(h, k, o).wait_recv()
        d4(h, k).start()

    dacts(0, lambda n, k: None)

    def err_grad(i):
        err_step(1, i)
        loop(NK, lambda k: grad_first(i, k))

    loop(NN, err_grad)
    loop(NK, lambda k: dp_step(0, k))
    dacts(1, grad_last)

    def gd_step(k):
        grad_last(last, k)
        for s in range(3):
            stv[k, s:s + 1, :] = jnp.sum(sacc[s, k].T, axis=0, keepdims=True)
        stv[k, 3:8, :] = jnp.zeros((5, KB), F32)
        dp_step(1, k)

    loop(NK, gd_step)

    e1 = rc(stv, rst, e1s, e1r, partner)
    e1.start()

    def e2(o):
        return rc(ss, rs2.at[o], e2s.at[o], e2r.at[o], zdev(o))

    loop(NK, lambda k: fwd_d(0, k))
    e1.wait_recv()
    ss[...] = stv[...] + rst[...]
    for o in range(1, Z):
        e2(o).start()

    loop(NK, lambda k: fwd_d(1, k))
    for o in range(1, Z):
        e2(o).wait_recv()

    def nd_copy(k):
        return pltpu.make_async_copy(
            nd_v.at[k], nd_o.at[pl.ds(pl.multiple_of(k * KB, KB), KB), :], out_sem.at[2 + k]
        )

    def nd_step(k):
        t = ss[k]
        for o in range(1, Z):
            t = t + rs2[o, k]
        ww, gw, gg = t[0:1], t[1:2], t[2:3]
        coef = gw / (ww + EPS)
        sq = (
            ww
            - 2.0 * STEP * (gw - coef * ww)
            + STEP * STEP * (gg - 2.0 * coef * gw + coef * coef * ww)
        )
        inv = 1.0 / jnp.sqrt(sq + EPS)
        up = jnp.broadcast_to((1.0 + STEP * coef) * inv, (128, KB)).T
        down = jnp.broadcast_to(STEP * inv, (128, KB)).T
        for n in range(NN):
            for j in range(NB // 128):
                wt = dec_v[n, pl.ds(pl.multiple_of(k * KB, KB), KB), j * 128:(j + 1) * 128]
                g = grad[n, k, :, j * 128:(j + 1) * 128]
                first = n * NB + j * 128
                nd_v[k, :, first:first + 128] = (wt.astype(F32) * up - g * down).astype(BF16)
        nd_copy(k).start()

    loop(NK, nd_step)
    for h in range(H):
        loop(NK, lambda k: d4in(h, k).wait_recv())
    dp_copy = pltpu.make_async_copy(dp, dp_o, out_sem.at[1])
    dp_copy.start()

    def drain(k):
        for h in range(H):
            for first in (a1, a4, d1, d4):
                first(h, k).wait_send()
            for o in range(1, Z):
                for each in (a2, a3, d2, d3):
                    each(h, k, o).wait_send()
        nd_copy(k).wait()

    def drain_n(n):
        for h in range(H):
            for o in range(1, NL):
                b1(h, n, o).wait_send()
                c1(h, n, o).wait_send()

    loop(NK, drain)
    loop(NN, drain_n)
    e1.wait_send()
    for o in range(1, Z):
        e2(o).wait_send()
    rt_copy.wait()
    dp_copy.wait()


def enc_grad_kernel(rt, dp, out):
    halves, blocks = dp.shape[:2]
    d = jnp.concatenate(
        [
            jnp.concatenate([dp[h, k] for k in range(blocks)], axis=1)
            for h in range(halves)
        ],
        axis=0,
    )
    out[...] = jnp.dot(rt[0], d, preferred_element_type=F32).astype(BF16)


def fused(W, NL, residuals, encoder, enc_bias, decoder, dec_bias):
    T, DW = residuals.shape
    LL = encoder.shape[1]
    Z = W // 2
    NK, NN = 4, 4
    KB, NB = LL // NK, DW // NN
    H = 2
    TH = T // H
    TB, TL = TH // Z, TH // NL
    KC = KB // 2
    V = pltpu.VMEM
    dma = pltpu.SemaphoreType.DMA
    sums, part, rows = (H, NK, 2, Z, TB, KC), (H, NK, Z, TB, KC), (H, NN, NL, TL, NB)
    one, per_z, per_l = (H, NK), (H, NK, Z), (H, NN, NL)
    scratch = [
        V((T, DW), BF16), V((NK, DW, KB), BF16), V((NN, LL, NB), BF16),
        V(sums, F32), V(part, F32), V(part, F32), V(part, F32), V((H, NK, TB, KC), F32),
        V(sums, BF16), V((H, NK, KB, TH), BF16), V((NN, NB, T), BF16),
        V(rows, F32), V(rows, BF16), V(rows, BF16), V(rows, BF16),
        V(sums, F32), V(sums, BF16), V(part, BF16), V(part, BF16), V(part, BF16), V(sums, BF16),
        V((NN, NK, KB, NB), F32), V((3, NK, KB, 128), F32),
        V((NK, 8, KB), F32), V((NK, 8, KB), F32), V((NK, 8, KB), F32), V((Z, NK, 8, KB), F32),
        V((NK, KB, DW), BF16),
        dma((1 + NK + NN,)), dma((2 + NK,)),
        dma(one), dma(one), dma(per_z), dma(per_z), dma(per_z), dma(per_z), dma(one), dma(one),
        dma(per_l), dma(per_l), dma(per_l), dma(per_l),
        dma(one), dma(one), dma(per_z), dma(per_z), dma(per_z), dma(per_z), dma(one), dma(one),
        dma, dma, dma((Z,)), dma((Z,)),
    ]
    hbm = pl.BlockSpec(memory_space=pl.ANY)
    vm = pl.BlockSpec(memory_space=pltpu.VMEM)
    new_decoder, dp, rt = pl.pallas_call(
        functools.partial(step_kernel, Z, NL, NK, NN),
        out_shape=(
            jax.ShapeDtypeStruct((LL, DW), BF16),
            jax.ShapeDtypeStruct(sums, BF16),
            jax.ShapeDtypeStruct((NN, NB, T), BF16),
        ),
        in_specs=[hbm, hbm, vm, hbm, vm],
        out_specs=(hbm, hbm, hbm),
        scratch_shapes=scratch,
        compiler_params=pltpu.CompilerParams(
            collective_id=0, has_side_effects=True, vmem_limit_bytes=60 * 2**20
        ),
        name="sae_step",
    )(residuals, encoder, enc_bias.reshape(NK, 2, 1, KC), decoder, dec_bias.reshape(NN, 1, NB))
    enc_grad = pl.pallas_call(
        enc_grad_kernel,
        grid=(NN,),
        out_shape=jax.ShapeDtypeStruct((DW, LL), BF16),
        in_specs=[
            pl.BlockSpec((1, NB, T), lambda i: (i, 0, 0)),
            pl.BlockSpec((H, 2 * NK, TH, KC), lambda i: (0, 0, 0, 0)),
        ],
        out_specs=pl.BlockSpec((NB, LL), lambda i: (i, 0)),
        compiler_params=pltpu.CompilerParams(vmem_limit_bytes=60 * 2**20),
        cost_estimate=pl.CostEstimate(
            flops=2 * T * DW * LL, bytes_accessed=2 * (T * DW + T * LL + DW * LL),
            transcendentals=0,
        ),
        name="enc_grad",
    )(rt, dp.reshape(H, 2 * NK, TH, KC))
    return enc_grad, new_decoder


def plain(residuals, encoder, enc_bias, decoder, dec_bias):
    tokens = residuals.shape[0]
    lat_count = lax.axis_size("lat")
    lat_rows = tokens // lat_count
    rows = residuals
    pre_rows = (
        lax.psum_scatter(
            jnp.dot(rows, encoder, preferred_element_type=jnp.float32),
            "width",
            scatter_dimension=0,
            tiled=True,
        )
        + enc_bias
    )
    active_rows = pre_rows > 0.0
    act_rows = jnp.maximum(pre_rows, 0.0).astype(jnp.bfloat16)
    acts = lax.all_gather(act_rows, "width", axis=0, tiled=True)
    rows = acts
    recon_rows = lax.psum_scatter(
        jnp.dot(rows, decoder, preferred_element_type=jnp.float32),
        "lat",
        scatter_dimension=0,
        tiled=True,
    )
    first = lax.axis_index("lat") * lat_rows
    own_rows = lax.dynamic_slice_in_dim(residuals, first, lat_rows, 0)
    error_part = (recon_rows + dec_bias - own_rows.astype(jnp.float32)).astype(jnp.bfloat16)
    error = lax.all_gather(error_part, "lat", axis=0, tiled=True)
    rows = error
    dacts_rows = (
        lax.psum_scatter(
            lax.dot_general(
                rows, decoder, (((1,), (1,)), ((), ())), preferred_element_type=jnp.float32
            ),
            "width",
            scatter_dimension=0,
            tiled=True,
        )
        + PENALTY
    )
    dpre_part = jnp.where(active_rows, dacts_rows, 0.0).astype(jnp.bfloat16)
    dpre = lax.all_gather(dpre_part, "width", axis=0, tiled=True)
    enc_grad = lax.dot_general(
        residuals, dpre, (((0,), (0,)), ((), ())), preferred_element_type=jnp.float32
    ).astype(jnp.bfloat16)
    grad = lax.dot_general(
        acts, error, (((0,), (0,)), ((), ())), preferred_element_type=jnp.float32
    )
    weight = decoder.astype(jnp.float32)
    ww, gw, gg = lax.psum(
        (
            jnp.sum(weight * weight, axis=1),
            jnp.sum(grad * weight, axis=1),
            jnp.sum(grad * grad, axis=1),
        ),
        "width",
    )
    coef_row = gw / (ww + EPS)
    coef = coef_row[:, None]
    moved = weight - STEP * (grad - coef * weight)
    squared = (
        ww
        - 2.0 * STEP * (gw - coef_row * ww)
        + STEP * STEP * (gg - 2.0 * coef_row * gw + coef_row * coef_row * ww)
    )
    new_decoder = (moved / jnp.sqrt(squared + EPS)[:, None]).astype(jnp.bfloat16)
    return (enc_grad, new_decoder)


def per_device(W, NL, residuals, encoder, enc_bias, decoder, dec_bias):
    T, DW = residuals.shape
    LL = encoder.shape[1]
    args = (residuals, encoder, enc_bias, decoder, dec_bias)
    fits = W % 2 == 0 and NL % 2 == 0 and T % (16 * W) == 0 and T % (32 * NL) == 0
    if fits and DW % 512 == 0 and LL % 1024 == 0 and T % 128 == 0:
        return fused(W, NL, *args)
    return plain(*args)


def solution(mesh):
    return jax.shard_map(
        functools.partial(per_device, mesh.shape["width"], mesh.shape["lat"]),
        mesh=mesh,
        in_specs=(P(None, "width"), P("width", "lat"), P("lat"), P("lat", "width"), P("width")),
        out_specs=(P("width", "lat"), P("lat", "width")),
        check_vma=False,
    )
```

profile of v0, /device:TPU:0, one launch (start us, length us, event | category | flops | bytes accessed | tf_op | source)
XLA Modules:
  0.0 93.8 jit_solution(4598186714890756634)
XLA Ops:
  0.6 82.5 %sae_step.1 = (bf16[1024,2048]{1,0:T(8,128)(2,1)}, bf16[2,4,2,4,48,128]{5,4,3,2,1,0:T(8,128)(2,1)}, bf16[4,512,384]{2,1,0:T(8,128)(2,1)}) custom-call(bf16[384,2048]{1,0:T(8,128)(2,1)} %res_h.1, bf16[2048,1024]{1,0:T(8,128)(2,1)} %enc_h.1, f32[4,2,1,128]{3,2,1,0:T(1,128)} %bitcast.5, bf16[1024,2048]{1,0:T(8,128)(2,1)} %dec_h.1, f32[4,1,512]{2,1,0:T(1,128)} %bitcast.4), custom_call_target="tpu_custom_call" | custom-call | tf_op jit(solution)/shard_map/sae_step/pallas_call | solution.py:471
  83.2 5.8 %enc_grad.1 = bf16[2048,1024]{1,0:T(8,128)(2,1)} custom-call(bf16[4,512,384]{2,1,0:T(8,128)(2,1)} %get-tuple-element.5.rt, bf16[2,8,192,128]{3,2,1,0:T(8,128)(2,1)} %bitcast.3), custom_call_target="tpu_custom_call" | custom-call | flops 1610612736 | bytes 6553600 | tf_op jit(solution)/shard_map/enc_grad/pallas_call | solution.py:486
  89.0 4.8 %copy.8 = bf16[1024,2048]{1,0:T(8,128)(2,1)} copy(bf16[1024,2048]{1,0:T(8,128)(2,1)} %get-tuple-element.11) | data formatting | bytes 8388608
where the time goes:
time: 94 us; the launch traced here: 93.8 us
  Pallas kernels  88.3 us (94%)
  local copies, waits for them, and re-layouts  4.79 us (5%)
    pallas_call x1, Pallas kernels, fused(): pl.pallas_call(functools.partial(step_kernel, Z, NL, NK, NN), out_shape=(...  82.5 us
    pallas_call x1, Pallas kernels, fused(): pl.pallas_call(enc_grad_kernel, grid=(NN,), out_shape=jax.ShapeDtypeStruc...  5.79 us
    unnamed x1, local copies, waits for them, and re-layouts  4.79 us

commit v1 on v0

--- a/solution.py
+++ b/solution.py
@@ -17,11 +17,11 @@
 
 def step_kernel(
     Z, NL, NK, NN,
-    res_h, enc_h, bias, dec_h, dbias,
-    nd_o, dp_o, rt_o,
-    res_v, enc_v, dec_v, stA, rxA, sA, rA, preS, acts, actsT, rt_v,
-    rf, sB, rB, err, dacc, sD, rxD, sS, rD, dp, grad, sacc, stv, rst, ss, rs2, nd_v,
-    in_sem, out_sem,
+    res_h, enc_h, bias_h, dec_h, dbias_h,
+    nd_v, dp, rt_v,
+    res_v, enc_v, dec_v, bias, dbias, stA, rxA, sA, rA, preS, acts, actsT,
+    rf, sB, rB, err, dacc, sD, rxD, sS, rD, grad, sacc, stv, rst, ss, rs2, st,
+    in_sem,
     a1s, a1r, a2s, a2r, a3s, a3r, a4s, a4r,
     bs, br, cs, cr,
     d1s, d1r, d2s, d2r, d3s, d3r, d4s, d4r,
@@ -72,8 +72,10 @@
 
     for k in range(NK):
         enc_copy(k).start()
-    for n in range(NN):
-        dec_copy(n).start()
+    c_bias = pltpu.make_async_copy(bias_h, bias, in_sem.at[1 + NK + NN])
+    c_dbias = pltpu.make_async_copy(dbias_h, dbias, in_sem.at[2 + NK + NN])
+    c_bias.start()
+    c_dbias.start()
 
     barrier = pltpu.get_barrier_semaphore()
     pl.semaphore_signal(barrier, inc=1, device_id=partner, device_id_type=MESH)
@@ -124,26 +126,38 @@
             a2(h, k, o).start()
 
     c_res.wait()
-    pl.semaphore_wait(barrier, 1 + (Z - 1) + (NL - 1))
+    for n in range(NN):
+        dec_copy(n).start()
 
     def pre_part(h, k):
         p = jnp.dot(res_v[h * TH:(h + 1) * TH, :], enc_v[k], preferred_element_type=F32)
         for j in range(2):
             stA[h, k, j] = p[:, j * KC:(j + 1) * KC].reshape(Z, TB, KC)
-        a1(h, k).start()
+
+    def pre_early(k):
+        enc_copy(k).wait()
+        pre_part(0, k)
 
     def pre_first(k):
         enc_copy(k).wait()
         pre_part(0, k)
-
-        @pl.when(k > 0)
-        def _():
-            combine_a(0, k - 1)
-
-    loop(NK, pre_first)
-    combine_a(0, NK - 1)
+        a1(0, k).start()
+        combine_a(0, k - EARLY)
+
+    def pre_next(h, k):
+        pre_part(h, k)
+        a1(h, k).start()
+
+    EARLY = NK // 2
+    loop(EARLY, pre_early)
+    pl.semaphore_wait(barrier, 1 + (Z - 1) + (NL - 1))
+    loop(EARLY, lambda k: a1(0, k).start())
+    lax.fori_loop(EARLY, NK, lambda k, _: (pre_first(k), 0)[1], 0)
+    lax.fori_loop(NK - EARLY, NK, lambda k, _: (combine_a(0, k), 0)[1], 0)
     for h in range(1, H):
-        loop(NK, lambda k: pre_part(h, k))
+        loop(NK, lambda k: pre_next(h, k))
+    c_bias.wait()
+    c_dbias.wait()
 
     def fwd_a(h, k):
         for o in range(1, Z):
@@ -169,8 +183,6 @@
         rt_v[n] = res_v[:, pl.ds(pl.multiple_of(n * NB, NB), NB)].T
 
     loop(NN, rt_step)
-    rt_copy = pltpu.make_async_copy(rt_v, rt_o, out_sem.at[0])
-    rt_copy.start()
 
     def b1(h, n, o):
         to = lat_to(o)
@@ -343,12 +355,15 @@
     loop(NK, lambda k: dp_step(0, k))
     dacts(1, grad_last)
 
+    def st_row(s, k, j):
+        return (k * 3 + s) * (KB // 128) + j
+
     def gd_step(k):
         grad_last(last, k)
         for s in range(3):
-            stv[k, s:s + 1, :] = jnp.sum(sacc[s, k].T, axis=0, keepdims=True)
-        stv[k, 3:8, :] = jnp.zeros((5, KB), F32)
-        dp_step(1, k)
+            total = jnp.sum(sacc[s, k].T, axis=0, keepdims=True)
+            for j in range(KB // 128):
+                stv[pl.ds(st_row(s, k, j), 1), :] = total[:, j * 128:(j + 1) * 128]
 
     loop(NK, gd_step)
 
@@ -363,21 +378,22 @@
     ss[...] = stv[...] + rst[...]
     for o in range(1, Z):
         e2(o).start()
-
-    loop(NK, lambda k: fwd_d(1, k))
+    loop(NK, lambda k: dp_step(1, k))
     for o in range(1, Z):
         e2(o).wait_recv()
 
-    def nd_copy(k):
-        return pltpu.make_async_copy(
-            nd_v.at[k], nd_o.at[pl.ds(pl.multiple_of(k * KB, KB), KB), :], out_sem.at[2 + k]
-        )
+    total = ss[...]
+    for o in range(1, Z):
+        total = total + rs2[o]
+    st[...] = total
 
     def nd_step(k):
-        t = ss[k]
-        for o in range(1, Z):
-            t = t + rs2[o, k]
-        ww, gw, gg = t[0:1], t[1:2], t[2:3]
+        ww, gw, gg = (
+            jnp.concatenate(
+                [st[pl.ds(st_row(s, k, j), 1), :] for j in range(KB // 128)], axis=1
+            )
+            for s in range(3)
+        )
         coef = gw / (ww + EPS)
         sq = (
             ww
@@ -393,13 +409,11 @@
                 g = grad[n, k, :, j * 128:(j + 1) * 128]
                 first = n * NB + j * 128
                 nd_v[k, :, first:first + 128] = (wt.astype(F32) * up - g * down).astype(BF16)
-        nd_copy(k).start()
 
     loop(NK, nd_step)
+    loop(NK, lambda k: fwd_d(1, k))
     for h in range(H):
         loop(NK, lambda k: d4in(h, k).wait_recv())
-    dp_copy = pltpu.make_async_copy(dp, dp_o, out_sem.at[1])
-    dp_copy.start()
 
     def drain(k):
         for h in range(H):
@@ -408,7 +422,6 @@
             for o in range(1, Z):
                 for each in (a2, a3, d2, d3):
                     each(h, k, o).wait_send()
-        nd_copy(k).wait()
 
     def drain_n(n):
         for h in range(H):
@@ -421,12 +434,18 @@
     e1.wait_send()
     for o in range(1, Z):
         e2(o).wait_send()
-    rt_copy.wait()
-    dp_copy.wait()
-
-
-def enc_grad_kernel(rt, dp, out):
+
+
+def finish_kernel(rt, dp, nd, eg_o, nd_o, eg_v, sem):
     halves, blocks = dp.shape[:2]
+    NN, NB = rt.shape[:2]
+    NK, KB = nd.shape[:2]
+    copies = [
+        pltpu.make_async_copy(nd.at[k], nd_o.at[k * KB:(k + 1) * KB, :], sem.at[k])
+        for k in range(NK)
+    ]
+    for copy in copies:
+        copy.start()
     d = jnp.concatenate(
         [
             jnp.concatenate([dp[h, k] for k in range(blocks)], axis=1)
@@ -434,7 +453,13 @@
         ],
         axis=0,
     )
-    out[...] = jnp.dot(rt[0], d, preferred_element_type=F32).astype(BF16)
+    for n in range(NN):
+        eg_v[n] = jnp.dot(rt[n], d, preferred_element_type=F32).astype(BF16)
+        copy = pltpu.make_async_copy(eg_v.at[n], eg_o.at[n * NB:(n + 1) * NB, :], sem.at[NK + n])
+        copy.start()
+        copies.append(copy)
+    for copy in copies:
+        copy.wait()
 
 
 def fused(W, NL, residuals, encoder, enc_bias, decoder, dec_bias):
@@ -450,56 +475,55 @@
     V = pltpu.VMEM
     dma = pltpu.SemaphoreType.DMA
     sums, part, rows = (H, NK, 2, Z, TB, KC), (H, NK, Z, TB, KC), (H, NN, NL, TL, NB)
+    stats = (3 * LL // 128, 128)
     one, per_z, per_l = (H, NK), (H, NK, Z), (H, NN, NL)
     scratch = [
         V((T, DW), BF16), V((NK, DW, KB), BF16), V((NN, LL, NB), BF16),
+        V((NK, 2, 1, KC), F32), V((NN, 1, NB), F32),
         V(sums, F32), V(part, F32), V(part, F32), V(part, F32), V((H, NK, TB, KC), F32),
-        V(sums, BF16), V((H, NK, KB, TH), BF16), V((NN, NB, T), BF16),
+        V(sums, BF16), V((H, NK, KB, TH), BF16),
         V(rows, F32), V(rows, BF16), V(rows, BF16), V(rows, BF16),
-        V(sums, F32), V(sums, BF16), V(part, BF16), V(part, BF16), V(part, BF16), V(sums, BF16),
+        V(sums, F32), V(sums, BF16), V(part, BF16), V(part, BF16), V(part, BF16),
         V((NN, NK, KB, NB), F32), V((3, NK, KB, 128), F32),
-        V((NK, 8, KB), F32), V((NK, 8, KB), F32), V((NK, 8, KB), F32), V((Z, NK, 8, KB), F32),
-        V((NK, KB, DW), BF16),
-        dma((1 + NK + NN,)), dma((2 + NK,)),
+        V(stats, F32), V(stats, F32), V(stats, F32), V((Z, *stats), F32), V(stats, F32),
+        dma((3 + NK + NN,)),
         dma(one), dma(one), dma(per_z), dma(per_z), dma(per_z), dma(per_z), dma(one), dma(one),
         dma(per_l), dma(per_l), dma(per_l), dma(per_l),
         dma(one), dma(one), dma(per_z), dma(per_z), dma(per_z), dma(per_z), dma(one), dma(one),
         dma, dma, dma((Z,)), dma((Z,)),
     ]
-    hbm = pl.BlockSpec(memory_space=pl.ANY)
+    hbm = pl.BlockSpec(memory_space=pltpu.HBM)
     vm = pl.BlockSpec(memory_space=pltpu.VMEM)
     new_decoder, dp, rt = pl.pallas_call(
         functools.partial(step_kernel, Z, NL, NK, NN),
         out_shape=(
-            jax.ShapeDtypeStruct((LL, DW), BF16),
-            jax.ShapeDtypeStruct(sums, BF16),
-            jax.ShapeDtypeStruct((NN, NB, T), BF16),
+            V((NK, KB, DW), BF16),
+            V(sums, BF16),
+            V((NN, NB, T), BF16),
         ),
-        in_specs=[hbm, hbm, vm, hbm, vm],
-        out_specs=(hbm, hbm, hbm),
+        in_specs=[hbm] * 5,
+        out_specs=(vm, vm, vm),
         scratch_shapes=scratch,
         compiler_params=pltpu.CompilerParams(
-            collective_id=0, has_side_effects=True, vmem_limit_bytes=60 * 2**20
+            collective_id=0, has_side_effects=True, vmem_limit_bytes=115 * 2**19
         ),
         name="sae_step",
     )(residuals, encoder, enc_bias.reshape(NK, 2, 1, KC), decoder, dec_bias.reshape(NN, 1, NB))
-    enc_grad = pl.pallas_call(
-        enc_grad_kernel,
-        grid=(NN,),
-        out_shape=jax.ShapeDtypeStruct((DW, LL), BF16),
-        in_specs=[
-            pl.BlockSpec((1, NB, T), lambda i: (i, 0, 0)),
-            pl.BlockSpec((H, 2 * NK, TH, KC), lambda i: (0, 0, 0, 0)),
-        ],
-        out_specs=pl.BlockSpec((NB, LL), lambda i: (i, 0)),
-        compiler_params=pltpu.CompilerParams(vmem_limit_bytes=60 * 2**20),
+    return pl.pallas_call(
+        finish_kernel,
+        out_shape=(
+            jax.ShapeDtypeStruct((DW, LL), BF16),
+            jax.ShapeDtypeStruct((LL, DW), BF16),
+        ),
+        in_specs=[vm, vm, vm],
+        out_specs=(hbm, hbm),
+        scratch_shapes=[V((NN, NB, LL), BF16), dma((NK + NN,))],
+        compiler_params=pltpu.CompilerParams(vmem_limit_bytes=30 * 2**20),
         cost_estimate=pl.CostEstimate(
-            flops=2 * T * DW * LL, bytes_accessed=2 * (T * DW + T * LL + DW * LL),
-            transcendentals=0,
+            flops=2 * T * DW * LL, bytes_accessed=4 * DW * LL, transcendentals=0,
         ),
-        name="enc_grad",
-    )(rt, dp.reshape(H, 2 * NK, TH, KC))
-    return enc_grad, new_decoder
+        name="finish",
+    )(rt, dp.reshape(H, 2 * NK, TH, KC), new_decoder)
 
 
 def plain(residuals, encoder, enc_bias, decoder, dec_bias):

time: 94 us -> 82.2 us (0.87)
  Pallas kernels: 88.3 us -> 81.4 us
  local copies, waits for them, and re-layouts: 4.79 us -> 0 us
    unnamed x1 -> x0, local copies, waits for them, and re-layouts: 4.79 us -> none
    pallas_call x1, Pallas kernels: 82.5 us -> 78 us  [fused(): pl.pallas_call(functools.partial(step_kernel, Z, NL, NK, NN), out_shape=(...]
    pallas_call x1, Pallas kernels: 5.79 us -> 3.39 us  [fused(): pl.pallas_call(finish_kernel, out_shape=(jax.ShapeDtypeStruct((DW, LL), B...]
where the time goes in v1:
time: 82.2 us; the launch traced here: 82 us
  Pallas kernels  81.4 us (99%)
    pallas_call x1, Pallas kernels, fused(): pl.pallas_call(functools.partial(step_kernel, Z, NL, NK, NN), out_shape=(...  78 us
    pallas_call x1, Pallas kernels, fused(): pl.pallas_call(finish_kernel, out_shape=(jax.ShapeDtypeStruct((DW, LL), B...  3.39 us

profile of v1, /device:TPU:0, one launch (start us, length us, event | category | flops | bytes accessed | tf_op | source)
XLA Modules:
  0.0 82.0 jit_solution(9564987803543252903)
XLA Ops:
  0.6 78.0 %sae_step.1 = (bf16[4,256,2048]{2,1,0:T(8,128)(2,1)S(1)}, bf16[2,4,2,4,48,128]{5,4,3,2,1,0:T(8,128)(2,1)S(1)}, bf16[4,512,384]{2,1,0:T(8,128)(2,1)S(1)}) custom-call(bf16[384,2048]{1,0:T(8,128)(2,1)} %res_h.1, bf16[2048,1024]{1,0:T(8,128)(2,1)} %enc_h.1, f32[4,2,1,128]{3,2,1,0:T(1,128)} %bitcast.5, bf16[1024,2048]{1,0:T(8,128)(2,1)} %dec_h.1, ...), custom_call_target="tpu_custom_call" | custom-call | tf_op jit(solution)/shard_map/sae_step/pallas_call | solution.py:497
  78.6 3.4 %finish.1 = (bf16[2048,1024]{1,0:T(8,128)(2,1)}, bf16[1024,2048]{1,0:T(8,128)(2,1)}) custom-call(bf16[4,512,384]{2,1,0:T(8,128)(2,1)S(1)} %get-tuple-element.5.rt, bf16[2,8,192,128]{3,2,1,0:T(8,128)(2,1)S(1)} %bitcast.3, bf16[4,256,2048]{2,1,0:T(8,128)(2,1)S(1)} %get-tuple-element.7.nd), custom_call_target="tpu_custom_call" | custom-call | flops 1610612736 | bytes 8388608 | tf_op jit(solution)/shard_map/finish/pallas_call | solution.py:512

commit v2 on v1

--- a/solution.py
+++ b/solution.py
@@ -19,13 +19,10 @@
     Z, NL, NK, NN,
     res_h, enc_h, bias_h, dec_h, dbias_h,
     nd_v, dp, rt_v,
-    res_v, enc_v, dec_v, bias, dbias, stA, rxA, sA, rA, preS, acts, actsT,
-    rf, sB, rB, err, dacc, sD, rxD, sS, rD, grad, sacc, stv, rst, ss, rs2, st,
-    in_sem,
-    a1s, a1r, a2s, a2r, a3s, a3r, a4s, a4r,
-    bs, br, cs, cr,
-    d1s, d1r, d2s, d2r, d3s, d3r, d4s, d4r,
-    e1s, e1r, e2s, e2r,
+    res_v, enc_v, dec_v, bias, dbias, stA, rxA, sA, qA, tA, rA, preS, acts, actsT,
+    rf, sB, fB, tB, rB, err, dacc, sD, rxD, sS, rD, grad, sacc, stv, rst, ss, rs2, st,
+    in_sem, sent,
+    a1r, a2r, a3r, a4r, br, cr, d1r, d2r, d3r, d4r, e1r, e2r,
 ):
     T, DW = res_v.shape
     H = acts.shape[0]
@@ -39,20 +36,39 @@
     pc = 1 - c
     partner = (z * 2 + pc, l)
 
+    side = z // 2
+    near, far_in, far_out = z + 1 - 2 * (z % 2), 2 - side, 3 - 3 * side
+    inner = (z + side) % 2
+
     def zdev(o):
         return ((z + o) % Z) * 2 + c, l
 
+    def on(other):
+        return other * 2 + c, l
+
     def lat_to(o):
         return ((l // 2 + o // 2) % (NL // 2)) * 2 + (l % 2 + o % 2) % 2
 
-    def lat_from(o):
-        return ((l // 2 + NL // 2 - o // 2) % (NL // 2)) * 2 + (l % 2 + o % 2) % 2
+    lx, ly, ld = lat_to(1), lat_to(2), lat_to(3)
 
     def rc(src, dst, ssem, rsem, dev):
         return pltpu.make_async_remote_copy(
             src_ref=src, dst_ref=dst, send_sem=ssem, recv_sem=rsem,
             device_id=dev, device_id_type=MESH,
         )
+
+    def arrived(ref, sem):
+        rc(ref, ref, sem, sem, partner).wait_recv()
+
+    def left(ref, sem):
+        rc(ref, ref, sem, sem, partner).wait_send()
+
+    A1, A2, A3, A4, B1, B2, C1, C2, D1, D2, D3, D4, E1, E2 = (
+        sent.at[i] for i in range(14)
+    )
+
+    def span(first, stop, f):
+        lax.fori_loop(first, stop, lambda i, _: (f(i), 0)[1], 0)
 
     def loop(n, f):
         lax.fori_loop(0, n, lambda i, _: (f(i), 0)[1], 0)
@@ -85,45 +101,64 @@
         pl.semaphore_signal(barrier, inc=1, device_id=(w, lat_to(o)), device_id_type=MESH)
 
     def a1(h, k):
-        return rc(stA.at[h, k, pc], rxA.at[h, k], a1s.at[h, k], a1r.at[h, k], partner)
-
-    def a2(h, k, o):
-        return rc(
-            sA.at[h, k, (z + o) % Z], rA.at[h, k, o], a2s.at[h, k, o], a2r.at[h, k, o], zdev(o)
-        )
-
-    def own_z(ref, ssem, rsem):
-        def send(h, k, o):
-            block = ref.at[h, k, c, z]
-            return rc(block, block, ssem.at[h, k, o], rsem.at[h, k, o], zdev(o))
-
-        def arrive(h, k, o):
-            block = ref.at[h, k, c, (z + Z - o) % Z]
-            return rc(block, block, ssem.at[h, k, o], rsem.at[h, k, o], zdev(o))
-
-        return send, arrive
+        return rc(stA.at[h, k, pc], rxA.at[h, k], A1, a1r.at[h, k], partner)
+
+    def a2(h, k, i):
+        src, dst, recv, to = (
+            (sA.at[h, k, near], rA.at[h, k, 0], 0, near),
+            (tA.at[h, k, 0], rA.at[h, k, 1], 0, far_in),
+            (tA.at[h, k, 1], rA.at[h, k, 1], 0, far_out),
+            (sA.at[h, k, far_in], qA.at[h, k, 0], 1, near),
+            (sA.at[h, k, far_out], qA.at[h, k, 1], 1, near),
+        )[i]
+        return rc(src, dst, A2, a2r.at[h, k, recv], on(to))
+
+    def a3(h, k, o):
+        block = acts.at[h, k, c, z]
+        return rc(block, block, A3, a3r.at[h, k], zdev(o))
+
+    def d3(h, k, o):
+        block = dp.at[h, k, c, z]
+        return rc(block, block, D3, d3r.at[h, k], zdev(o))
 
     def own_core(ref, ssem, rsem):
         def send(h, k):
             block = ref.at[h, k, c]
-            return rc(block, block, ssem.at[h, k], rsem.at[h, k], partner)
+            return rc(block, block, ssem, rsem.at[h, k], partner)
 
         def arrive(h, k):
-            block = ref.at[h, k, pc]
-            return rc(block, block, ssem.at[h, k], rsem.at[h, k], partner)
+            arrived(ref.at[h, k, pc], rsem.at[h, k])
 
         return send, arrive
 
-    a3, a3in = own_z(acts, a3s, a3r)
-    a4, a4in = own_core(acts, a4s, a4r)
-    d3, d3in = own_z(dp, d3s, d3r)
-    d4, d4in = own_core(dp, d4s, d4r)
+    a4, a4in = own_core(acts, A4, a4r)
+    d4, d4in = own_core(dp, D4, d4r)
 
     def combine_a(h, k):
         a1(h, k).wait_recv()
         sA[h, k] = stA[h, k, c] + rxA[h, k]
-        for o in range(1, Z):
-            a2(h, k, o).start()
+
+        @pl.when(inner == 0)
+        def _():
+            a2(h, k, 3).start()
+            a2(h, k, 4).start()
+
+        @pl.when(inner == 1)
+        def _():
+            a2(h, k, 0).start()
+
+    def near_a(h, k):
+        @pl.when(inner == 0)
+        def _():
+            a2(h, k, 0).start()
+
+    def relay_a(h, k):
+        @pl.when(inner == 1)
+        def _():
+            arrived(qA.at[h, k], a2r.at[h, k, 1])
+            for i, block in enumerate((far_in, far_out)):
+                tA[h, k, i] = sA[h, k, block] + qA[h, k, i]
+                a2(h, k, 1 + i).start()
 
     c_res.wait()
     for n in range(NN):
@@ -154,47 +189,75 @@
     loop(EARLY, lambda k: a1(0, k).start())
     lax.fori_loop(EARLY, NK, lambda k, _: (pre_first(k), 0)[1], 0)
     lax.fori_loop(NK - EARLY, NK, lambda k, _: (combine_a(0, k), 0)[1], 0)
+    loop(NK, lambda k: near_a(0, k))
     for h in range(1, H):
         loop(NK, lambda k: pre_next(h, k))
+
+    def second_a(k):
+        combine_a(1, k)
+        near_a(1, k)
+
+    span(0, EARLY, second_a)
     c_bias.wait()
     c_dbias.wait()
 
     def fwd_a(h, k):
-        for o in range(1, Z):
-            a3in(h, k, o).wait_recv()
+        arrived(acts.at[h, k, c, 1:Z], a3r.at[h, k])
         a4(h, k).start()
 
     def act_step(h, k):
-        for o in range(1, Z):
-            a2(h, k, o).wait_recv()
-        pre = sA[h, k, z]
-        for o in range(1, Z):
-            pre = pre + rA[h, k, o]
+        arrived(rA.at[h, k], a2r.at[h, k, 0])
+        pre = (sA[h, k, z] + rA[h, k, 0]) + rA[h, k, 1]
         pre = pre + bias[k, c]
         preS[h, k] = pre
         acts[h, k, c, z] = jnp.maximum(pre, 0.0).astype(BF16)
         for o in range(1, Z):
             a3(h, k, o).start()
 
+    loop(NK, lambda k: relay_a(0, k))
     loop(NK, lambda k: act_step(0, k))
-    loop(NK, lambda k: combine_a(1, k))
+    span(EARLY, NK, second_a)
 
     def rt_step(n):
         rt_v[n] = res_v[:, pl.ds(pl.multiple_of(n * NB, NB), NB)].T
 
     loop(NN, rt_step)
-
-    def b1(h, n, o):
-        to = lat_to(o)
-        return rc(sB.at[h, n, to], rB.at[h, n, o], bs.at[h, n, o], br.at[h, n, o], (w, to))
-
-    def c1(h, n, o):
+    span(0, EARLY, lambda k: relay_a(1, k))
+
+    halves = (slice(0, NB // 2), slice(NB // 2, NB))
+
+    def b1(h, n, i):
+        to, block, half, dst = (
+            (lx, ld, 1, fB.at[h, n, 0]),
+            (ly, ld, 0, fB.at[h, n, 1]),
+            (lx, lx, 1, rB.at[h, n, 0]),
+            (ly, ly, 0, rB.at[h, n, 1]),
+        )[i]
+        return rc(sB.at[h, n, block, :, halves[half]], dst, B1, br.at[h, n, i // 2], (w, to))
+
+    def b2(h, n, i):
+        return rc(
+            tB.at[h, n, i], rB.at[h, n, 2 + i], B2, br.at[h, n, 1], (w, (ly, lx)[i]),
+        )
+
+    def relay_b(h, n):
+        arrived(fB.at[h, n], br.at[h, n, 0])
+        for i, block, half in ((0, ly, 1), (1, lx, 0)):
+            tB[h, n, i] = (rf[h, n, block, :, halves[half]] + fB[h, n, i].astype(F32)).astype(BF16)
+            b2(h, n, i).start()
+
+    def c1(h, n, i):
         block = err.at[h, n, l]
-        return rc(block, block, cs.at[h, n, o], cr.at[h, n, o], (w, lat_to(o)))
-
-    def c1in(h, n, o):
-        block = err.at[h, n, lat_from(o)]
-        return rc(block, block, cs.at[h, n, o], cr.at[h, n, o], (w, lat_to(o)))
+        return rc(block, block, C1, cr.at[h, n, 0], (w, (lx, ly)[i]))
+
+    def c2(h, n, i):
+        block = err.at[h, n, (lx, ly)[i], :, halves[1 - i]]
+        return rc(block, block, C2, cr.at[h, n, 1], (w, (ly, lx)[i]))
+
+    def fwd_c(h, n):
+        arrived(err.at[h, n, 0:2], cr.at[h, n, 0])
+        for i in range(2):
+            c2(h, n, i).start()
 
     def rec_step(h, n):
         a = jnp.concatenate(
@@ -203,37 +266,41 @@
         r = jnp.dot(a, dec_v[n], preferred_element_type=F32).reshape(NL, TL, NB)
         rf[h, n] = r
         sB[h, n] = r.astype(BF16)
-        for o in range(1, NL):
-            b1(h, n, o).start()
+        for i in range(4):
+            b1(h, n, i).start()
 
     def at_step(h, k):
         a = jnp.concatenate([acts[h, k, j].reshape(TH, KC) for j in range(2)], axis=1)
         actsT[h, k] = a.T
 
     def err_step(h, n):
-        for o in range(1, NL):
-            b1(h, n, o).wait_recv()
-        r = rf[h, n, l]
-        for o in range(1, NL):
-            r = r + rB[h, n, o].astype(F32)
-        own = res_v[
-            pl.ds(pl.multiple_of(h * TH + l * TL, TL), TL),
-            pl.ds(pl.multiple_of(n * NB, NB), NB),
-        ]
-        err[h, n, l] = (r + dbias[n] - own.astype(F32)).astype(BF16)
-        for o in range(1, NL):
-            c1(h, n, o).start()
-
-    def recon(h):
-        loop(NK, lambda k: fwd_a(h, k))
-        if h == 0:
-            for n in range(NN):
-                dec_copy(n).wait()
-        loop(NK, lambda k: a4in(h, k).wait_recv())
-        loop(NN, lambda n: rec_step(h, n))
-        loop(NK, lambda k: at_step(h, k))
-
-    recon(0)
+        arrived(rB.at[h, n], br.at[h, n, 1])
+        for half in range(2):
+            cols = halves[half]
+            r = rf[h, n, l, :, cols]
+            for j in (1 - half, 3 - half):
+                r = r + rB[h, n, j].astype(F32)
+            own = res_v[
+                pl.ds(pl.multiple_of(h * TH + l * TL, TL), TL),
+                pl.ds(pl.multiple_of(n * NB + half * (NB // 2), NB // 2), NB // 2),
+            ]
+            err[h, n, l, :, cols] = (r + dbias[n, :, cols] - own.astype(F32)).astype(BF16)
+        for i in range(2):
+            c1(h, n, i).start()
+
+    loop(EARLY, lambda k: fwd_a(0, k))
+
+    def fwd_relay(k):
+        relay_a(1, k)
+        fwd_a(0, k)
+
+    span(EARLY, NK, fwd_relay)
+    for n in range(NN):
+        dec_copy(n).wait()
+    loop(NK, lambda k: a4in(0, k))
+    loop(NN, lambda n: rec_step(0, n))
+    loop(NK, lambda k: act_step(1, k))
+    loop(NK, lambda k: at_step(0, k))
 
     def zero_step(k):
         for s in range(3):
@@ -241,12 +308,17 @@
 
     loop(NK, zero_step)
 
-    def err_act(i):
-        err_step(0, i)
-        act_step(1, i)
-
-    loop(NK, err_act)
-    recon(1)
+    def rec_fwd(n):
+        rec_step(1, n)
+        fwd_c(0, n)
+
+    loop(NN, lambda n: relay_b(0, n))
+    span(0, NN // 2, lambda n: err_step(0, n))
+    span(NN // 2, NN, lambda n: err_step(0, n))
+    loop(NK, lambda k: fwd_a(1, k))
+    loop(NK, lambda k: a4in(1, k))
+    loop(NN, rec_fwd)
+    loop(NK, lambda k: at_step(1, k))
 
     def dec_rows(n, k):
         return dec_v[n, pl.ds(pl.multiple_of(k * KB, KB), KB), :]
@@ -275,15 +347,14 @@
             sacc[s, k] += part
 
     def err_wait(h, n):
-        for o in range(1, NL):
-            c1in(h, n, o).wait_recv()
+        arrived(err.at[h, n, 0], cr.at[h, n, 1])
 
     def d1(h, k):
-        return rc(sD.at[h, k, pc], rxD.at[h, k], d1s.at[h, k], d1r.at[h, k], partner)
+        return rc(sD.at[h, k, pc], rxD.at[h, k], D1, d1r.at[h, k], partner)
 
     def d2(h, k, o):
         return rc(
-            sS.at[h, k, (z + o) % Z], rD.at[h, k, o], d2s.at[h, k, o], d2r.at[h, k, o], zdev(o)
+            sS.at[h, k, (z + o) % Z], rD.at[h, k, o], D2, d2r.at[h, k], zdev(o)
         )
 
     def combine_d(h, k):
@@ -310,10 +381,6 @@
             sD[h, k, j] = v.astype(BF16)
         d1(h, k).start()
 
-        @pl.when(k > 0)
-        def _():
-            combine_d(h, k - 1)
-
     def dacts(h, beside):
         def step(n):
             err_wait(h, n)
@@ -324,15 +391,21 @@
 
             loop(NK, k_step)
 
+            if h == 0 and not isinstance(n, int):
+                relay_b(1, n - 1)
+
         step(0)
         lax.fori_loop(1, last, lambda n, _: (step(n), 0)[1], 0)
         err_wait(h, last)
+        if h == 0:
+            relay_b(1, last - 1)
         loop(NK, lambda k: d_step(h, k))
-        combine_d(h, NK - 1)
+        if h == 0:
+            relay_b(1, last)
+        loop(NK, lambda k: combine_d(h, k))
 
     def dp_step(h, k):
-        for o in range(1, Z):
-            d2(h, k, o).wait_recv()
+        arrived(rD.at[h, k, 1:Z], d2r.at[h, k])
         v = dacc[h, k, c, z]
         for o in range(1, Z):
             v = v + rD[h, k, o].astype(F32)
@@ -341,8 +414,7 @@
             d3(h, k, o).start()
 
     def fwd_d(h, k):
-        for o in range(1, Z):
-            d3in(h, k, o).wait_recv()
+        arrived(dp.at[h, k, c, 1:Z], d3r.at[h, k])
         d4(h, k).start()
 
     dacts(0, lambda n, k: None)
@@ -351,8 +423,13 @@
         err_step(1, i)
         loop(NK, lambda k: grad_first(i, k))
 
-    loop(NN, err_grad)
+    loop(2, err_grad)
+    for i in range(2, NN):
+        err_grad(i)
+        fwd_c(1, i - 2)
+    fwd_c(1, NN - 2)
     loop(NK, lambda k: dp_step(0, k))
+    fwd_c(1, NN - 1)
     dacts(1, grad_last)
 
     def st_row(s, k, j):
@@ -367,11 +444,11 @@
 
     loop(NK, gd_step)
 
-    e1 = rc(stv, rst, e1s, e1r, partner)
+    e1 = rc(stv, rst, E1, e1r, partner)
     e1.start()
 
     def e2(o):
-        return rc(ss, rs2.at[o], e2s.at[o], e2r.at[o], zdev(o))
+        return rc(ss, rs2.at[o], E2, e2r, zdev(o))
 
     loop(NK, lambda k: fwd_d(0, k))
     e1.wait_recv()
@@ -379,8 +456,7 @@
     for o in range(1, Z):
         e2(o).start()
     loop(NK, lambda k: dp_step(1, k))
-    for o in range(1, Z):
-        e2(o).wait_recv()
+    arrived(rs2.at[1:Z], e2r)
 
     total = ss[...]
     for o in range(1, Z):
@@ -413,28 +489,15 @@
     loop(NK, nd_step)
     loop(NK, lambda k: fwd_d(1, k))
     for h in range(H):
-        loop(NK, lambda k: d4in(h, k).wait_recv())
-
-    def drain(k):
-        for h in range(H):
-            for first in (a1, a4, d1, d4):
-                first(h, k).wait_send()
-            for o in range(1, Z):
-                for each in (a2, a3, d2, d3):
-                    each(h, k, o).wait_send()
-
-    def drain_n(n):
-        for h in range(H):
-            for o in range(1, NL):
-                b1(h, n, o).wait_send()
-                c1(h, n, o).wait_send()
-
-    loop(NK, drain)
-    loop(NN, drain_n)
-    e1.wait_send()
-    for o in range(1, Z):
-        e2(o).wait_send()
-
+        loop(NK, lambda k: d4in(h, k))
+
+    for ref, sem in (
+        (rxA, A1), (sA.at[:, :, 1:Z], A2), (acts.at[:, :, 0, 1:Z], A3),
+        (acts.at[:, :, 0], A4), (rB, B1), (tB, B2), (err.at[:, :, 0:2], C1), (err.at[:, :, 0], C2),
+        (sD.at[:, :, 0], D1), (sS.at[:, :, 1:Z], D2), (dp.at[:, :, 0, 1:Z], D3),
+        (dp.at[:, :, 0], D4), (ss, E1), (rs2.at[1:Z], E2),
+    ):
+        left(ref, sem)
 
 def finish_kernel(rt, dp, nd, eg_o, nd_o, eg_v, sem):
     halves, blocks = dp.shape[:2]
@@ -476,21 +539,22 @@
     dma = pltpu.SemaphoreType.DMA
     sums, part, rows = (H, NK, 2, Z, TB, KC), (H, NK, Z, TB, KC), (H, NN, NL, TL, NB)
     stats = (3 * LL // 128, 128)
-    one, per_z, per_l = (H, NK), (H, NK, Z), (H, NN, NL)
+    one, two = (H, NK), (H, NK, 2)
+    half, pair = (TL, NB // 2), (H, NK, 2, TB, KC)
     scratch = [
         V((T, DW), BF16), V((NK, DW, KB), BF16), V((NN, LL, NB), BF16),
         V((NK, 2, 1, KC), F32), V((NN, 1, NB), F32),
-        V(sums, F32), V(part, F32), V(part, F32), V(part, F32), V((H, NK, TB, KC), F32),
+        V(sums, F32), V(part, F32), V(part, F32), V(pair, F32), V(pair, F32), V(pair, F32),
+        V((H, NK, TB, KC), F32),
         V(sums, BF16), V((H, NK, KB, TH), BF16),
-        V(rows, F32), V(rows, BF16), V(rows, BF16), V(rows, BF16),
+        V(rows, F32), V(rows, BF16), V((H, NN, 2, *half), BF16), V((H, NN, 2, *half), BF16),
+        V((H, NN, 4, *half), BF16), V(rows, BF16),
         V(sums, F32), V(sums, BF16), V(part, BF16), V(part, BF16), V(part, BF16),
         V((NN, NK, KB, NB), F32), V((3, NK, KB, 128), F32),
         V(stats, F32), V(stats, F32), V(stats, F32), V((Z, *stats), F32), V(stats, F32),
-        dma((3 + NK + NN,)),
-        dma(one), dma(one), dma(per_z), dma(per_z), dma(per_z), dma(per_z), dma(one), dma(one),
-        dma(per_l), dma(per_l), dma(per_l), dma(per_l),
-        dma(one), dma(one), dma(per_z), dma(per_z), dma(per_z), dma(per_z), dma(one), dma(one),
-        dma, dma, dma((Z,)), dma((Z,)),
+        dma((3 + NK + NN,)), dma((14,)),
+        dma(one), dma(two), dma(one), dma(one), dma((H, NN, 2)), dma((H, NN, 2)),
+        dma(one), dma(one), dma(one), dma(one), dma, dma,
     ]
     hbm = pl.BlockSpec(memory_space=pltpu.HBM)
     vm = pl.BlockSpec(memory_space=pltpu.VMEM)
@@ -599,7 +663,7 @@
     T, DW = residuals.shape
     LL = encoder.shape[1]
     args = (residuals, encoder, enc_bias, decoder, dec_bias)
-    fits = W % 2 == 0 and NL % 2 == 0 and T % (16 * W) == 0 and T % (32 * NL) == 0
+    fits = W == 8 and NL == 4 and T % (16 * W) == 0 and T % (32 * NL) == 0
     if fits and DW % 512 == 0 and LL % 1024 == 0 and T % 128 == 0:
         return fused(W, NL, *args)
     return plain(*args)

time: 82.2 us -> 76.7 us (0.933)
  Pallas kernels: 81.4 us -> 75.9 us
    pallas_call x1, Pallas kernels: 78 us -> 72.5 us  [fused(): pl.pallas_call(functools.partial(step_kernel, Z, NL, NK, NN), out_shape=(...]
where the time goes in v2:
time: 76.7 us; the launch traced here: 76.5 us
  Pallas kernels  75.9 us (99%)
    pallas_call x1, Pallas kernels, fused(): pl.pallas_call(functools.partial(step_kernel, Z, NL, NK, NN), out_shape=(...  72.5 us
    pallas_call x1, Pallas kernels, fused(): pl.pallas_call(finish_kernel, out_shape=(jax.ShapeDtypeStruct((DW, LL), B...  3.39 us

profile of v2, /device:TPU:0, one launch (start us, length us, event | category | flops | bytes accessed | tf_op | source)
XLA Modules:
  0.0 76.5 jit_solution(4572404608283586568)
XLA Ops:
  0.6 72.5 %sae_step.1 = (bf16[4,256,2048]{2,1,0:T(8,128)(2,1)S(1)}, bf16[2,4,2,4,48,128]{5,4,3,2,1,0:T(8,128)(2,1)S(1)}, bf16[4,512,384]{2,1,0:T(8,128)(2,1)S(1)}) custom-call(bf16[384,2048]{1,0:T(8,128)(2,1)} %res_h.1, bf16[2048,1024]{1,0:T(8,128)(2,1)} %enc_h.1, f32[4,2,1,128]{3,2,1,0:T(1,128)} %bitcast.5, bf16[1024,2048]{1,0:T(8,128)(2,1)} %dec_h.1, ...), custom_call_target="tpu_custom_call" | custom-call | tf_op jit(solution)/shard_map/sae_step/pallas_call | solution.py:561
  73.2 3.4 %finish.1 = (bf16[2048,1024]{1,0:T(8,128)(2,1)}, bf16[1024,2048]{1,0:T(8,128)(2,1)}) custom-call(bf16[4,512,384]{2,1,0:T(8,128)(2,1)S(1)} %get-tuple-element.5.rt, bf16[2,8,192,128]{3,2,1,0:T(8,128)(2,1)S(1)} %bitcast.3, bf16[4,256,2048]{2,1,0:T(8,128)(2,1)S(1)} %get-tuple-element.7.nd), custom_call_target="tpu_custom_call" | custom-call | flops 1610612736 | bytes 8388608 | tf_op jit(solution)/shard_map/finish/pallas_call | solution.py:576

commit v3 on v2

--- a/solution.py
+++ b/solution.py
@@ -190,14 +190,13 @@
     lax.fori_loop(EARLY, NK, lambda k, _: (pre_first(k), 0)[1], 0)
     lax.fori_loop(NK - EARLY, NK, lambda k, _: (combine_a(0, k), 0)[1], 0)
     loop(NK, lambda k: near_a(0, k))
-    for h in range(1, H):
-        loop(NK, lambda k: pre_next(h, k))
-
-    def second_a(k):
-        combine_a(1, k)
-        near_a(1, k)
-
-    span(0, EARLY, second_a)
+    def second_a(h, k):
+        combine_a(h, k)
+        near_a(h, k)
+
+    loop(NK, lambda k: pre_next(1, k))
+    loop(NK, lambda k: second_a(1, k))
+    loop(NK, lambda k: pre_next(2, k))
     c_bias.wait()
     c_dbias.wait()
 
@@ -216,13 +215,13 @@
 
     loop(NK, lambda k: relay_a(0, k))
     loop(NK, lambda k: act_step(0, k))
-    span(EARLY, NK, second_a)
+    loop(NK, lambda k: second_a(2, k))
 
     def rt_step(n):
         rt_v[n] = res_v[:, pl.ds(pl.multiple_of(n * NB, NB), NB)].T
 
     loop(NN, rt_step)
-    span(0, EARLY, lambda k: relay_a(1, k))
+    loop(NK, lambda k: relay_a(1, k))
 
     halves = (slice(0, NB // 2), slice(NB // 2, NB))
 
@@ -271,7 +270,7 @@
 
     def at_step(h, k):
         a = jnp.concatenate([acts[h, k, j].reshape(TH, KC) for j in range(2)], axis=1)
-        actsT[h, k] = a.T
+        actsT[k, :, h * TH:(h + 1) * TH] = a.T
 
     def err_step(h, n):
         arrived(rB.at[h, n], br.at[h, n, 1])
@@ -288,18 +287,13 @@
         for i in range(2):
             c1(h, n, i).start()
 
-    loop(EARLY, lambda k: fwd_a(0, k))
-
-    def fwd_relay(k):
-        relay_a(1, k)
-        fwd_a(0, k)
-
-    span(EARLY, NK, fwd_relay)
+    loop(NK, lambda k: fwd_a(0, k))
     for n in range(NN):
         dec_copy(n).wait()
     loop(NK, lambda k: a4in(0, k))
     loop(NN, lambda n: rec_step(0, n))
     loop(NK, lambda k: act_step(1, k))
+    loop(NK, lambda k: relay_a(2, k))
     loop(NK, lambda k: at_step(0, k))
 
     def zero_step(k):
@@ -308,17 +302,15 @@
 
     loop(NK, zero_step)
 
-    def rec_fwd(n):
-        rec_step(1, n)
-        fwd_c(0, n)
-
     loop(NN, lambda n: relay_b(0, n))
-    span(0, NN // 2, lambda n: err_step(0, n))
-    span(NN // 2, NN, lambda n: err_step(0, n))
+    loop(NN, lambda n: err_step(0, n))
     loop(NK, lambda k: fwd_a(1, k))
     loop(NK, lambda k: a4in(1, k))
-    loop(NN, rec_fwd)
+    loop(NN, lambda n: rec_step(1, n))
+    loop(NK, lambda k: act_step(2, k))
+    loop(NN, lambda n: fwd_c(0, n))
     loop(NK, lambda k: at_step(1, k))
+    loop(NN, lambda n: relay_b(1, n))
 
     def dec_rows(n, k):
         return dec_v[n, pl.ds(pl.multiple_of(k * KB, KB), KB), :]
@@ -331,12 +323,12 @@
 
     def grad_first(n, k):
         grad[n, k] = jnp.dot(
-            actsT[0, k], err[0, n].reshape(TH, NB), preferred_element_type=F32
+            actsT[k, :, 0:2 * TH], err[0:2, n].reshape(2 * TH, NB), preferred_element_type=F32
         )
 
     def grad_last(n, k):
         g = grad[n, k] + jnp.dot(
-            actsT[1, k], err[1, n].reshape(TH, NB), preferred_element_type=F32
+            actsT[k, :, 2 * TH:T], err[2, n].reshape(TH, NB), preferred_element_type=F32
         )
         grad[n, k] = g
         wt = dec_rows(n, k).astype(F32)
@@ -381,28 +373,15 @@
             sD[h, k, j] = v.astype(BF16)
         d1(h, k).start()
 
-    def dacts(h, beside):
-        def step(n):
-            err_wait(h, n)
-
-            def k_step(k):
-                dacts_add(h, n, k)
-                beside(n, k)
-
-            loop(NK, k_step)
-
-            if h == 0 and not isinstance(n, int):
-                relay_b(1, n - 1)
-
-        step(0)
-        lax.fori_loop(1, last, lambda n, _: (step(n), 0)[1], 0)
+    def dacts(h, n):
+        err_wait(h, n)
+        for k in range(NK):
+            dacts_add(h, n, k)
+
+    def d_steps(h):
         err_wait(h, last)
-        if h == 0:
-            relay_b(1, last - 1)
-        loop(NK, lambda k: d_step(h, k))
-        if h == 0:
-            relay_b(1, last)
-        loop(NK, lambda k: combine_d(h, k))
+        for k in range(NK):
+            d_step(h, k)
 
     def dp_step(h, k):
         arrived(rD.at[h, k, 1:Z], d2r.at[h, k])
@@ -417,20 +396,63 @@
         arrived(dp.at[h, k, c, 1:Z], d3r.at[h, k])
         d4(h, k).start()
 
-    dacts(0, lambda n, k: None)
-
-    def err_grad(i):
-        err_step(1, i)
-        loop(NK, lambda k: grad_first(i, k))
-
-    loop(2, err_grad)
-    for i in range(2, NN):
-        err_grad(i)
-        fwd_c(1, i - 2)
-    fwd_c(1, NN - 2)
+    def grad_n(n):
+        for k in range(NK):
+            grad_first(n, k)
+
+    def err_dacts(n):
+        err_step(2, n)
+        dacts(1, n)
+
+    loop(NK, lambda k: fwd_a(2, k))
+    err_step(1, 0)
+    dacts(0, 0)
+    err_step(1, 1)
+    loop(NK, lambda k: a4in(2, k))
+
+    def err_rec(n):
+        rec_step(2, n - NN // 2)
+        err_step(1, n)
+
+    span(NN // 2, NN, err_rec)
+    span(NN - NN // 2, NN, lambda n: rec_step(2, n))
+
+    def dacts_fwd(n):
+        dacts(0, n)
+        fwd_c(1, n - 1)
+
+    span(1, last, dacts_fwd)
+    d_steps(0)
+    span(NN - 2, NN, lambda n: fwd_c(1, n))
+    loop(NK, lambda k: combine_d(0, k))
+    relay_b(2, 0)
+    loop(NK, lambda k: at_step(2, k))
+    span(1, NN, lambda n: relay_b(2, n))
+    err_dacts(0)
+    span(1, last, err_dacts)
+    err_step(2, last)
+    d_steps(1)
+    fwd_c(2, 0)
     loop(NK, lambda k: dp_step(0, k))
-    fwd_c(1, NN - 1)
-    dacts(1, grad_last)
+    loop(NK, lambda k: combine_d(1, k))
+    fwd_c(2, 1)
+    grad_n(0)
+    fwd_c(2, 2)
+    grad_n(1)
+    fwd_c(2, 3)
+    grad_n(2)
+    dacts(2, 0)
+    grad_n(3)
+    span(1, last, lambda n: dacts(2, n))
+    d_steps(2)
+    loop(NK, lambda k: combine_d(2, k))
+    loop(NK, lambda k: dp_step(1, k))
+
+    def grads_last(n):
+        for k in range(NK):
+            grad_last(n, k)
+
+    span(0, last, grads_last)
 
     def st_row(s, k, j):
         return (k * 3 + s) * (KB // 128) + j
@@ -442,7 +464,8 @@
             for j in range(KB // 128):
                 stv[pl.ds(st_row(s, k, j), 1), :] = total[:, j * 128:(j + 1) * 128]
 
-    loop(NK, gd_step)
+    for k in range(NK):
+        gd_step(k)
 
     e1 = rc(stv, rst, E1, e1r, partner)
     e1.start()
@@ -455,7 +478,8 @@
     ss[...] = stv[...] + rst[...]
     for o in range(1, Z):
         e2(o).start()
-    loop(NK, lambda k: dp_step(1, k))
+    loop(NK, lambda k: dp_step(2, k))
+    loop(NK, lambda k: fwd_d(1, k))
     arrived(rs2.at[1:Z], e2r)
 
     total = ss[...]
@@ -487,7 +511,7 @@
                 nd_v[k, :, first:first + 128] = (wt.astype(F32) * up - g * down).astype(BF16)
 
     loop(NK, nd_step)
-    loop(NK, lambda k: fwd_d(1, k))
+    loop(NK, lambda k: fwd_d(2, k))
     for h in range(H):
         loop(NK, lambda k: d4in(h, k))
 
@@ -531,7 +555,7 @@
     Z = W // 2
     NK, NN = 4, 4
     KB, NB = LL // NK, DW // NN
-    H = 2
+    H = 3
     TH = T // H
     TB, TL = TH // Z, TH // NL
     KC = KB // 2
@@ -546,7 +570,7 @@
         V((NK, 2, 1, KC), F32), V((NN, 1, NB), F32),
         V(sums, F32), V(part, F32), V(part, F32), V(pair, F32), V(pair, F32), V(pair, F32),
         V((H, NK, TB, KC), F32),
-        V(sums, BF16), V((H, NK, KB, TH), BF16),
+        V(sums, BF16), V((NK, KB, T), BF16),
         V(rows, F32), V(rows, BF16), V((H, NN, 2, *half), BF16), V((H, NN, 2, *half), BF16),
         V((H, NN, 4, *half), BF16), V(rows, BF16),
         V(sums, F32), V(sums, BF16), V(part, BF16), V(part, BF16), V(part, BF16),
@@ -663,7 +687,7 @@
     T, DW = residuals.shape
     LL = encoder.shape[1]
     args = (residuals, encoder, enc_bias, decoder, dec_bias)
-    fits = W == 8 and NL == 4 and T % (16 * W) == 0 and T % (32 * NL) == 0
+    fits = W == 8 and NL == 4 and T % (48 * NL) == 0
     if fits and DW % 512 == 0 and LL % 1024 == 0 and T % 128 == 0:
         return fused(W, NL, *args)
     return plain(*args)

time: 76.7 us -> 74.4 us (0.970)
  Pallas kernels: 75.9 us -> 73.7 us
    pallas_call x1, Pallas kernels: 72.5 us -> 70.3 us  [fused(): pl.pallas_call(functools.partial(step_kernel, Z, NL, NK, NN), out_shape=(...]
where the time goes in v3:
time: 74.4 us; the launch traced here: 74.3 us
  Pallas kernels  73.7 us (99%)
    pallas_call x1, Pallas kernels, fused(): pl.pallas_call(functools.partial(step_kernel, Z, NL, NK, NN), out_shape=(...  70.3 us
    pallas_call x1, Pallas kernels, fused(): pl.pallas_call(finish_kernel, out_shape=(jax.ShapeDtypeStruct((DW, LL), B...  3.39 us

profile of v3, /device:TPU:0, one launch (start us, length us, event | category | flops | bytes accessed | tf_op | source)
XLA Modules:
  0.0 74.3 jit_solution(3139743477607647317)
XLA Ops:
  0.6 70.3 %sae_step.1 = (bf16[4,256,2048]{2,1,0:T(8,128)(2,1)S(1)}, bf16[3,4,2,4,32,128]{5,4,3,2,1,0:T(8,128)(2,1)S(1)}, bf16[4,512,384]{2,1,0:T(8,128)(2,1)S(1)}) custom-call(bf16[384,2048]{1,0:T(8,128)(2,1)} %res_h.1, bf16[2048,1024]{1,0:T(8,128)(2,1)} %enc_h.1, f32[4,2,1,128]{3,2,1,0:T(1,128)} %bitcast.5, bf16[1024,2048]{1,0:T(8,128)(2,1)} %dec_h.1, ...), custom_call_target="tpu_custom_call" | custom-call | tf_op jit(solution)/shard_map/sae_step/pallas_call | solution.py:585
  70.9 3.4 %finish.1 = (bf16[2048,1024]{1,0:T(8,128)(2,1)}, bf16[1024,2048]{1,0:T(8,128)(2,1)}) custom-call(bf16[4,512,384]{2,1,0:T(8,128)(2,1)S(1)} %get-tuple-element.5.rt, bf16[3,8,128,128]{3,2,1,0:T(8,128)(2,1)S(1)} %bitcast.3, bf16[4,256,2048]{2,1,0:T(8,128)(2,1)S(1)} %get-tuple-element.7.nd), custom_call_target="tpu_custom_call" | custom-call | flops 1610612736 | bytes 8388608 | tf_op jit(solution)/shard_map/finish/pallas_call | solution.py:600

commit v4 on v3

--- a/solution.py
+++ b/solution.py
@@ -22,7 +22,7 @@
     res_v, enc_v, dec_v, bias, dbias, stA, rxA, sA, qA, tA, rA, preS, acts, actsT,
     rf, sB, fB, tB, rB, err, dacc, sD, rxD, sS, rD, grad, sacc, stv, rst, ss, rs2, st,
     in_sem, sent,
-    a1r, a2r, a3r, a4r, br, cr, d1r, d2r, d3r, d4r, e1r, e2r,
+    r1, r2, r3, r4, rx, e1r, e2r,
 ):
     T, DW = res_v.shape
     H = acts.shape[0]
@@ -63,8 +63,8 @@
     def left(ref, sem):
         rc(ref, ref, sem, sem, partner).wait_send()
 
-    A1, A2, A3, A4, B1, B2, C1, C2, D1, D2, D3, D4, E1, E2 = (
-        sent.at[i] for i in range(14)
+    A1, A2, A3, A4, B1, B2, C1, C2, D1, D2, D3, D3F, D3L, D4, E1, E2 = (
+        sent.at[i] for i in range(16)
     )
 
     def span(first, stop, f):
@@ -101,7 +101,7 @@
         pl.semaphore_signal(barrier, inc=1, device_id=(w, lat_to(o)), device_id_type=MESH)
 
     def a1(h, k):
-        return rc(stA.at[h, k, pc], rxA.at[h, k], A1, a1r.at[h, k], partner)
+        return rc(stA.at[h, k, pc], rxA.at[h, k], A1, r1.at[h, k], partner)
 
     def a2(h, k, i):
         src, dst, recv, to = (
@@ -111,15 +111,29 @@
             (sA.at[h, k, far_in], qA.at[h, k, 0], 1, near),
             (sA.at[h, k, far_out], qA.at[h, k, 1], 1, near),
         )[i]
-        return rc(src, dst, A2, a2r.at[h, k, recv], on(to))
+        return rc(src, dst, A2, r2.at[h, k, recv], on(to))
 
     def a3(h, k, o):
         block = acts.at[h, k, c, z]
-        return rc(block, block, A3, a3r.at[h, k], zdev(o))
+        return rc(block, block, A3, r3.at[h, k, 0], zdev(o))
 
     def d3(h, k, o):
         block = dp.at[h, k, c, z]
-        return rc(block, block, D3, d3r.at[h, k], zdev(o))
+        return rc(block, block, D3L, r3.at[h, k, 0], zdev(o))
+
+    def d3_near(h, k, i):
+        block, recv, to, sem = (
+            (z, 0, near, D3), (z, 1, far_in, D3), (far_in, 1, near, D3F), (far_out, 1, near, D3F)
+        )[i]
+        block = dp.at[h, k, c, block]
+        return rc(block, block, sem, r3.at[h, k, recv], on(to))
+
+    def pass_d(h, k):
+        @pl.when(inner == 1)
+        def _():
+            arrived(dp.at[h, k, c, 0:2], r3.at[h, k, 1])
+            d3_near(h, k, 2).start()
+            d3_near(h, k, 3).start()
 
     def own_core(ref, ssem, rsem):
         def send(h, k):
@@ -131,8 +145,8 @@
 
         return send, arrive
 
-    a4, a4in = own_core(acts, A4, a4r)
-    d4, d4in = own_core(dp, D4, d4r)
+    a4, a4in = own_core(acts, A4, r4)
+    d4, d4in = own_core(dp, D4, r4)
 
     def combine_a(h, k):
         a1(h, k).wait_recv()
@@ -155,7 +169,7 @@
     def relay_a(h, k):
         @pl.when(inner == 1)
         def _():
-            arrived(qA.at[h, k], a2r.at[h, k, 1])
+            arrived(qA.at[h, k], r2.at[h, k, 1])
             for i, block in enumerate((far_in, far_out)):
                 tA[h, k, i] = sA[h, k, block] + qA[h, k, i]
                 a2(h, k, 1 + i).start()
@@ -201,11 +215,11 @@
     c_dbias.wait()
 
     def fwd_a(h, k):
-        arrived(acts.at[h, k, c, 1:Z], a3r.at[h, k])
+        arrived(acts.at[h, k, c, 1:Z], r3.at[h, k, 0])
         a4(h, k).start()
 
     def act_step(h, k):
-        arrived(rA.at[h, k], a2r.at[h, k, 0])
+        arrived(rA.at[h, k], r2.at[h, k, 0])
         pre = (sA[h, k, z] + rA[h, k, 0]) + rA[h, k, 1]
         pre = pre + bias[k, c]
         preS[h, k] = pre
@@ -223,6 +237,7 @@
     loop(NN, rt_step)
     loop(NK, lambda k: relay_a(1, k))
 
+    last_n = NN - 1
     halves = (slice(0, NB // 2), slice(NB // 2, NB))
 
     def b1(h, n, i):
@@ -232,29 +247,29 @@
             (lx, lx, 1, rB.at[h, n, 0]),
             (ly, ly, 0, rB.at[h, n, 1]),
         )[i]
-        return rc(sB.at[h, n, block, :, halves[half]], dst, B1, br.at[h, n, i // 2], (w, to))
+        return rc(sB.at[h, n, block, :, halves[half]], dst, B1, rx.at[h, n, i // 2], (w, to))
 
     def b2(h, n, i):
         return rc(
-            tB.at[h, n, i], rB.at[h, n, 2 + i], B2, br.at[h, n, 1], (w, (ly, lx)[i]),
+            tB.at[h, n, i], rB.at[h, n, 2 + i], B2, rx.at[h, n, 1], (w, (ly, lx)[i]),
         )
 
     def relay_b(h, n):
-        arrived(fB.at[h, n], br.at[h, n, 0])
+        arrived(fB.at[h, n], rx.at[h, n, 0])
         for i, block, half in ((0, ly, 1), (1, lx, 0)):
             tB[h, n, i] = (rf[h, n, block, :, halves[half]] + fB[h, n, i].astype(F32)).astype(BF16)
             b2(h, n, i).start()
 
     def c1(h, n, i):
         block = err.at[h, n, l]
-        return rc(block, block, C1, cr.at[h, n, 0], (w, (lx, ly)[i]))
+        return rc(block, block, C1, rx.at[h, n, 0], (w, (lx, ly)[i]))
 
     def c2(h, n, i):
         block = err.at[h, n, (lx, ly)[i], :, halves[1 - i]]
-        return rc(block, block, C2, cr.at[h, n, 1], (w, (ly, lx)[i]))
+        return rc(block, block, C2, rx.at[h, n, 1], (w, (ly, lx)[i]))
 
     def fwd_c(h, n):
-        arrived(err.at[h, n, 0:2], cr.at[h, n, 0])
+        arrived(err.at[h, n, 0:2], rx.at[h, n, 0])
         for i in range(2):
             c2(h, n, i).start()
 
@@ -273,7 +288,7 @@
         actsT[k, :, h * TH:(h + 1) * TH] = a.T
 
     def err_step(h, n):
-        arrived(rB.at[h, n], br.at[h, n, 1])
+        arrived(rB.at[h, n], rx.at[h, n, 1])
         for half in range(2):
             cols = halves[half]
             r = rf[h, n, l, :, cols]
@@ -297,20 +312,25 @@
     loop(NK, lambda k: at_step(0, k))
 
     def zero_step(k):
-        for s in range(3):
+        for s in range(1, 3):
             sacc[s, k] = jnp.zeros(sacc.shape[2:], F32)
 
     loop(NK, zero_step)
 
     loop(NN, lambda n: relay_b(0, n))
-    loop(NN, lambda n: err_step(0, n))
+    span(0, NN // 2, lambda n: err_step(0, n))
     loop(NK, lambda k: fwd_a(1, k))
+    span(NN // 2, last_n, lambda n: err_step(0, n))
     loop(NK, lambda k: a4in(1, k))
-    loop(NN, lambda n: rec_step(1, n))
+    span(0, NN // 2, lambda n: rec_step(1, n))
+    err_step(0, last_n)
+    span(NN // 2, NN, lambda n: rec_step(1, n))
     loop(NK, lambda k: act_step(2, k))
-    loop(NN, lambda n: fwd_c(0, n))
+    span(0, last_n, lambda n: fwd_c(0, n))
+    span(0, NN // 2, lambda n: relay_b(1, n))
+    fwd_c(0, last_n)
     loop(NK, lambda k: at_step(1, k))
-    loop(NN, lambda n: relay_b(1, n))
+    span(NN // 2, NN, lambda n: relay_b(1, n))
 
     def dec_rows(n, k):
         return dec_v[n, pl.ds(pl.multiple_of(k * KB, KB), KB), :]
@@ -332,21 +352,21 @@
         )
         grad[n, k] = g
         wt = dec_rows(n, k).astype(F32)
-        for s, prod in enumerate((wt * wt, g * wt, g * g)):
+        for s, prod in ((1, g * wt), (2, g * g)):
             part = prod[:, 0:128]
             for j in range(1, NB // 128):
                 part = part + prod[:, j * 128:(j + 1) * 128]
             sacc[s, k] += part
 
     def err_wait(h, n):
-        arrived(err.at[h, n, 0], cr.at[h, n, 1])
+        arrived(err.at[h, n, 0], rx.at[h, n, 1])
 
     def d1(h, k):
-        return rc(sD.at[h, k, pc], rxD.at[h, k], D1, d1r.at[h, k], partner)
+        return rc(sD.at[h, k, pc], rxD.at[h, k], D1, r1.at[h, k], partner)
 
     def d2(h, k, o):
         return rc(
-            sS.at[h, k, (z + o) % Z], rD.at[h, k, o], D2, d2r.at[h, k], zdev(o)
+            sS.at[h, k, (z + o) % Z], rD.at[h, k, o], D2, r2.at[h, k, 0], zdev(o)
         )
 
     def combine_d(h, k):
@@ -384,21 +404,41 @@
             d_step(h, k)
 
     def dp_step(h, k):
-        arrived(rD.at[h, k, 1:Z], d2r.at[h, k])
+        arrived(rD.at[h, k, 1:Z], r2.at[h, k, 0])
         v = dacc[h, k, c, z]
         for o in range(1, Z):
             v = v + rD[h, k, o].astype(F32)
         dp[h, k, c, z] = jnp.where(preS[h, k] > 0.0, v + PENALTY, 0.0).astype(BF16)
-        for o in range(1, Z):
-            d3(h, k, o).start()
+        if h < 2:
+            d3_near(h, k, 0).start()
+            d3_near(h, k, 1).start()
+        else:
+            for o in range(1, Z):
+                d3(h, k, o).start()
 
     def fwd_d(h, k):
-        arrived(dp.at[h, k, c, 1:Z], d3r.at[h, k])
+        if h < 2:
+            @pl.when(inner == 0)
+            def _():
+                arrived(dp.at[h, k, c, 0:2], r3.at[h, k, 1])
+
+            arrived(dp.at[h, k, c, 0], r3.at[h, k, 0])
+        else:
+            arrived(dp.at[h, k, c, 1:Z], r3.at[h, k, 0])
         d4(h, k).start()
 
     def grad_n(n):
         for k in range(NK):
             grad_first(n, k)
+
+    def ww_step(k):
+        total = jnp.zeros(sacc.shape[2:], F32)
+        for n in range(NN):
+            wt = dec_rows(n, k).astype(F32)
+            prod = wt * wt
+            for j in range(NB // 128):
+                total = total + prod[:, j * 128:(j + 1) * 128]
+        sacc[0, k] = total
 
     def err_dacts(n):
         err_step(2, n)
@@ -422,31 +462,36 @@
         fwd_c(1, n - 1)
 
     span(1, last, dacts_fwd)
+    relay_b(2, 0)
     d_steps(0)
-    span(NN - 2, NN, lambda n: fwd_c(1, n))
+    fwd_c(1, NN - 2)
+    span(1, NN - 2, lambda n: relay_b(2, n))
+    fwd_c(1, NN - 1)
     loop(NK, lambda k: combine_d(0, k))
-    relay_b(2, 0)
+    relay_b(2, NN - 2)
     loop(NK, lambda k: at_step(2, k))
-    span(1, NN, lambda n: relay_b(2, n))
+    relay_b(2, NN - 1)
+    loop(NK, ww_step)
     err_dacts(0)
     span(1, last, err_dacts)
     err_step(2, last)
     d_steps(1)
     fwd_c(2, 0)
+    loop(NK, lambda k: combine_d(1, k))
     loop(NK, lambda k: dp_step(0, k))
-    loop(NK, lambda k: combine_d(1, k))
     fwd_c(2, 1)
     grad_n(0)
     fwd_c(2, 2)
     grad_n(1)
     fwd_c(2, 3)
     grad_n(2)
+    grad_n(3)
     dacts(2, 0)
-    grad_n(3)
     span(1, last, lambda n: dacts(2, n))
     d_steps(2)
     loop(NK, lambda k: combine_d(2, k))
     loop(NK, lambda k: dp_step(1, k))
+    loop(NK, lambda k: pass_d(0, k))
 
     def grads_last(n):
         for k in range(NK):
@@ -473,13 +518,13 @@
     def e2(o):
         return rc(ss, rs2.at[o], E2, e2r, zdev(o))
 
-    loop(NK, lambda k: fwd_d(0, k))
     e1.wait_recv()
     ss[...] = stv[...] + rst[...]
     for o in range(1, Z):
         e2(o).start()
     loop(NK, lambda k: dp_step(2, k))
-    loop(NK, lambda k: fwd_d(1, k))
+    loop(NK, lambda k: pass_d(1, k))
+    loop(NK, lambda k: fwd_d(0, k))
     arrived(rs2.at[1:Z], e2r)
 
     total = ss[...]
@@ -511,6 +556,7 @@
                 nd_v[k, :, first:first + 128] = (wt.astype(F32) * up - g * down).astype(BF16)
 
     loop(NK, nd_step)
+    loop(NK, lambda k: fwd_d(1, k))
     loop(NK, lambda k: fwd_d(2, k))
     for h in range(H):
         loop(NK, lambda k: d4in(h, k))
@@ -518,10 +564,14 @@
     for ref, sem in (
         (rxA, A1), (sA.at[:, :, 1:Z], A2), (acts.at[:, :, 0, 1:Z], A3),
         (acts.at[:, :, 0], A4), (rB, B1), (tB, B2), (err.at[:, :, 0:2], C1), (err.at[:, :, 0], C2),
-        (sD.at[:, :, 0], D1), (sS.at[:, :, 1:Z], D2), (dp.at[:, :, 0, 1:Z], D3),
+        (sD.at[:, :, 0], D1), (sS.at[:, :, 1:Z], D2), (dp.at[0:2, :, 0, 0:2], D3), (dp.at[2, :, 0, 1:Z], D3L),
         (dp.at[:, :, 0], D4), (ss, E1), (rs2.at[1:Z], E2),
     ):
         left(ref, sem)
+
+    @pl.when(inner == 1)
+    def _():
+        left(dp.at[0:2, :, 0, 0:2], D3F)
 
 def finish_kernel(rt, dp, nd, eg_o, nd_o, eg_v, sem):
     halves, blocks = dp.shape[:2]
@@ -576,9 +626,8 @@
         V(sums, F32), V(sums, BF16), V(part, BF16), V(part, BF16), V(part, BF16),
         V((NN, NK, KB, NB), F32), V((3, NK, KB, 128), F32),
         V(stats, F32), V(stats, F32), V(stats, F32), V((Z, *stats), F32), V(stats, F32),
-        dma((3 + NK + NN,)), dma((14,)),
-        dma(one), dma(two), dma(one), dma(one), dma((H, NN, 2)), dma((H, NN, 2)),
-        dma(one), dma(one), dma(one), dma(one), dma, dma,
+        dma((3 + NK + NN,)), dma((16,)),
+        dma(one), dma(two), dma(two), dma(one), dma((H, NN, 2)), dma, dma,
     ]
     hbm = pl.BlockSpec(memory_space=pltpu.HBM)
     vm = pl.BlockSpec(memory_space=pltpu.VMEM)

time: 74.4 us -> 71.7 us (0.964)
  Pallas kernels: 73.7 us -> 70.9 us
    pallas_call x1, Pallas kernels: 70.3 us -> 67.5 us  [fused(): pl.pallas_call(functools.partial(step_kernel, Z, NL, NK, NN), out_shape=(...]
where the time goes in v4:
time: 71.7 us; the launch traced here: 71.6 us
  Pallas kernels  70.9 us (99%)
    pallas_call x1, Pallas kernels, fused(): pl.pallas_call(functools.partial(step_kernel, Z, NL, NK, NN), out_shape=(...  67.5 us
    pallas_call x1, Pallas kernels, fused(): pl.pallas_call(finish_kernel, out_shape=(jax.ShapeDtypeStruct((DW, LL), B...  3.39 us

profile of v4, /device:TPU:0, one launch (start us, length us, event | category | flops | bytes accessed | tf_op | source)
XLA Modules:
  0.0 71.6 jit_solution(14604317291304894509)
XLA Ops:
  0.6 67.5 %sae_step.1 = (bf16[4,256,2048]{2,1,0:T(8,128)(2,1)S(1)}, bf16[3,4,2,4,32,128]{5,4,3,2,1,0:T(8,128)(2,1)S(1)}, bf16[4,512,384]{2,1,0:T(8,128)(2,1)S(1)}) custom-call(bf16[384,2048]{1,0:T(8,128)(2,1)} %res_h.1, bf16[2048,1024]{1,0:T(8,128)(2,1)} %enc_h.1, f32[4,2,1,128]{3,2,1,0:T(1,128)} %bitcast.5, bf16[1024,2048]{1,0:T(8,128)(2,1)} %dec_h.1, ...), custom_call_target="tpu_custom_call" | custom-call | tf_op jit(solution)/shard_map/sae_step/pallas_call | solution.py:634
  68.2 3.4 %finish.1 = (bf16[2048,1024]{1,0:T(8,128)(2,1)}, bf16[1024,2048]{1,0:T(8,128)(2,1)}) custom-call(bf16[4,512,384]{2,1,0:T(8,128)(2,1)S(1)} %get-tuple-element.5.rt, bf16[3,8,128,128]{3,2,1,0:T(8,128)(2,1)S(1)} %bitcast.3, bf16[4,256,2048]{2,1,0:T(8,128)(2,1)S(1)} %get-tuple-element.7.nd), custom_call_target="tpu_custom_call" | custom-call | flops 1610612736 | bytes 8388608 | tf_op jit(solution)/shard_map/finish/pallas_call | solution.py:649
